TPU v7x, 8 devices: a whole 2x2x1 slice. The times are simulated.
8 devices in a mesh: dp: 2 (over y, z), tp: 4 (over x, core).
Axes of the slice: x: 2, y: 2, z: 1, core: 2. Of those that a mesh axis runs over, the one named last changes fastest.
Arguments:
- x: bfloat16 [4096, 5120], P('dp'), parts along dimension 0
- w_gate: bfloat16 [5120, 17920], P(None, 'tp')
- w_up: bfloat16 [5120, 17920], P(None, 'tp')
- w_down: bfloat16 [17920, 5120], P('tp')
Outputs:
- output: bfloat16 [4096, 5120], P('dp'), parts along dimension 0
There are 2 independent parts. A program takes and returns all parts, laid end to end along the dimension named above; an argument that names none is the same for every part.
All inputs are finite; a program needn't handle non-finite values.
Results may differ from a plain program's by a relative error of at most 0.016.
Values are sent between devices in bfloat16 or wider.
A program may use at most 2 GiB of HBM per device.

v0:
```python
import jax
import jax.numpy as jnp
from jax import lax
from jax.sharding import PartitionSpec as P


def solution(mesh):
    def step(x, w_gate, w_up, w_down):
        gate = jnp.dot(x, w_gate, preferred_element_type=jnp.float32)
        up = jnp.dot(x, w_up, preferred_element_type=jnp.float32)
        hidden = (jax.nn.silu(gate) * up).astype(jnp.bfloat16)
        term = jnp.dot(hidden, w_down, preferred_element_type=jnp.float32).astype(jnp.bfloat16)
        return lax.psum(term, "tp")

    return jax.shard_map(
        step,
        mesh=mesh,
        in_specs=(P("dp", None), P(None, "tp"), P(None, "tp"), P("tp", None)),
        out_specs=P("dp", None),
        check_vma=False,
    )
```

profile of v0, /device:TPU:0, one launch (start us, length us, event | category | flops | bytes accessed | tf_op | source)
XLA Modules:
  0.0 721.1 jit_solution(12578185272405347474)
XLA Ops:
  6.5 0.0 all-reduce.2.cloned.1.call-start
  6.5 112.5 %fusion = f32[2048,4480]{1,0:T(8,128)} fusion(bf16[2048,5120]{1,0:T(8,128)(2,1)} %param.4, bf16[5120,4480]{1,0:T(8,128)(2,1)} %param.5), kind=kOutput, calls=%fused_computation.2 | convolution fusion | flops 93952409600 | bytes 103546880 | tf_op jit(solution)/shard_map/dot_general | solution.py:9
  119.0 117.3 %multiply_convert_fusion = bf16[2048,4480]{1,0:T(8,128)(2,1)} fusion(f32[2048,4480]{1,0:T(8,128)} %fusion, bf16[2048,5120]{1,0:T(8,128)(2,1)} %param.4, bf16[5120,4480]{1,0:T(8,128)(2,1)} %param.6), kind=kOutput, calls=%fused_computation | convolution fusion | flops 94007459840 | bytes 121896960 | tf_op jit(solution)/shard_map/dot_general | solution.py:10
  236.3 107.1 %convolution_convert_fusion = bf16[2048,5120]{1,0:T(8,128)(2,1)} fusion(bf16[2048,4480]{1,0:T(8,128)(2,1)} %multiply_convert_fusion, bf16[4480,5120]{1,0:T(8,128)(2,1)} %param.7), kind=kOutput, calls=%fused_computation.1 | convolution fusion | flops 93962895360 | bytes 85196800 | tf_op jit(solution)/shard_map/dot_general | solution.py:12
  343.4 0.0 all-reduce.2.cloned.1.call-update
  343.4 353.5 %all-reduce.2.cloned.1.call-done = bf16[2048,5120]{1,0:T(8,128)(2,1)} async-done(((bf16[2048,5120]{1,0:T(8,128)(2,1)}), bf16[2048,5120]{1,0:T(8,128)(2,1)}) %all-reduce.2.cloned.1.call-update) | async-done | bytes 20971536 | tf_op jit(solution)/shard_map/psum | solution.py:13
  696.9 17.3 %copy.6 = bf16[2048,5120]{1,0:T(8,128)(2,1)} copy(bf16[2048,5120]{1,0:T(8,128)(2,1)} %all-reduce.2.cloned.1.call-done) | data formatting | bytes 41943040
Async XLA Ops:
  6.5 690.4 %all-reduce.2.cloned.1.call-start = ((), (), s32[]{:S(2)}) async-start(), calls=%async_computation | async-start | bytes 41943040 | tf_op jit(solution)/shard_map/psum | solution.py:13
Sparse Core Ops, SparseCore 0:
  343.5 353.3 all-reduce.1
where the time goes:
time: 721 us
  waiting for transfers between devices  354 us (49%)
  matrix products  337 us (47%)
  local copies, waits for them, and re-layouts  17.3 us (2%)
  between operations  13.4 us (2%)
    psum x1, waiting for transfers between devices, step(): return lax.psum(term, 'tp')  354 us
    dot_general x1, matrix products, step(): up = jnp.dot(x, w_up, preferred_element_type=jnp.float32)  117 us
    dot_general x1, matrix products, step(): gate = jnp.dot(x, w_gate, preferred_element_type=jnp.float32)  112 us
    dot_general x1, matrix products, step(): jnp.dot(hidden, w_down, preferred_element_type=jnp.float32)  107 us
    unnamed x1, local copies, waits for them, and re-layouts  17.3 us
  transfers between devices with their start and end apart: 1, of which 1 were waited for; matrix products, arithmetic and copies ran while one was open for 0% of the time, Pallas kernels for 0%

commit v1 on v0

v1 whole, which is shorter than its diff:
```python
import jax
import jax.numpy as jnp
from jax import lax
from jax.experimental import pallas as pl
from jax.experimental.pallas import tpu as pltpu
from jax.sharding import PartitionSpec as P

BF = jnp.bfloat16
F32 = jnp.float32
CHUNK = 512
G = 640
T = 1280
Q = 640


def kernel(x, wg, wu, wd, y, xb, hb, wb, own, snd, rcv, csum, crcv, yb,
           xsem, wsem, psend, precv, csend, crecv, ylocal, ysend, yrecv, pfree, cfree):
    rows, depth = x.shape
    width = wg.shape[1]
    m, half = CHUNK, CHUNK // 2
    chunks, ng, nd, nq = rows // m, width // G, depth // T, depth // Q
    tp = lax.axis_index("tp")
    core = lax.rem(tp, 2)
    partner = tp + 1 - 2 * core
    peer = lax.rem(tp + 2, 4)

    def remote(src, dst, send, recv, to):
        return pltpu.make_async_remote_copy(
            src_ref=src, dst_ref=dst, send_sem=send, recv_sem=recv,
            device_id={"tp": to}, device_id_type=pl.DeviceIdType.MESH)

    def signal(sem, to):
        pl.semaphore_signal(sem, inc=1, device_id={"tp": to}, device_id_type=pl.DeviceIdType.MESH)

    def cols(i, size):
        return pl.ds(pl.multiple_of(i * size, 128), size)

    def rows_at(i, size):
        return pl.ds(pl.multiple_of(i, 16), size)

    def x_copies(ch):
        return [pltpu.make_async_copy(x.at[rows_at(ch * m + who * half, half), :],
                                      xb.at[pl.ds(k * half, half), :], xsem.at[k])
                for k, who in enumerate((1 - core, core))]

    def gu_copies(j, slot):
        return [pltpu.make_async_copy(w.at[:, cols(j, G)], wb.at[slot, :, pl.ds(k * G, G)], wsem.at[slot, k])
                for k, w in enumerate((wg, wu))]

    def d_copies(n, slot):
        return [pltpu.make_async_copy(wd.at[:, cols(n, T)], wb.at[slot, pl.ds(0, width), pl.ds(0, T)], wsem.at[slot, 0])]

    def start(copies):
        for c in copies:
            c.start()

    def wait(copies):
        for c in copies:
            c.wait()

    def term_copy(n):
        return remote(snd.at[n], rcv.at[n], psend.at[n], precv.at[n], partner)

    def sum_copy(q):
        return remote(csum.at[q], crcv.at[q], csend.at[q], crecv.at[q], peer)

    def y_copies(ch, q, s):
        there = y.at[rows_at(ch * m + core * half, half), cols(q, Q)]
        return (pltpu.make_async_copy(yb.at[s], there, ylocal.at[s]),
                remote(yb.at[s], there, ysend.at[s], yrecv.at[ch * nq + q], partner))

    def chip_sum(ch, n):
        term_copy(n).wait()
        s = own[lax.rem(n, 2)] + rcv[n].astype(F32)
        for k in range(T // Q):
            csum[n * (T // Q) + k] = s[:, k * Q:(k + 1) * Q].astype(BF)

        @pl.when(ch < chunks - 1)
        def _():
            signal(pfree, partner)

        @pl.when(ch > 0)
        def _():
            pl.semaphore_wait(cfree, T // Q)
        for k in range(T // Q):
            sum_copy(n * (T // Q) + k).start()

    def finish(ch, q):
        sum_copy(q).wait()
        s = lax.rem(q, 2)

        @pl.when(ch * nq + q >= 2)
        def _():
            here, there = y_copies(ch, q, s)
            here.wait()
            there.wait_send()
        yb[s] = (csum[q].astype(F32) + crcv[q].astype(F32)).astype(BF)
        for c in y_copies(ch, q, s):
            c.start()

        @pl.when(ch < chunks - 1)
        def _():
            signal(cfree, peer)

    start(x_copies(0))
    start(gu_copies(0, 0))
    barrier = pltpu.get_barrier_semaphore()
    signal(barrier, partner)
    signal(barrier, peer)
    pl.semaphore_wait(barrier, 2)

    def chunk(ch, _):
        base = ch * (ng + nd)
        wait(x_copies(ch))

        def gate_up(j, _):
            slot = lax.rem(base + j, 2)
            wait(gu_copies(j, slot))

            @pl.when(j < ng - 1)
            def _():
                start(gu_copies(j + 1, 1 - slot))

            @pl.when(j == ng - 1)
            def _():
                start(d_copies(0, 1 - slot))

            def unit(lo, size):
                w = jnp.concatenate([wb[slot, :, lo:lo + size], wb[slot, :, G + lo:G + lo + size]], axis=1)
                acc = jnp.dot(xb[...], w, preferred_element_type=F32)
                hb[:, pl.ds(pl.multiple_of(j * G + lo, 128), size)] = (
                    jax.nn.silu(acc[:, :size]) * acc[:, size:]).astype(BF)

            unit(0, 384)

            @pl.when((ch > 0) & (j == 0))
            def _():
                chip_sum(ch - 1, nd - 1)

            @pl.when(ch > 0)
            def _():
                finish(ch - 1, j)
            unit(384, 256)
            return 0

        lax.fori_loop(0, ng, gate_up, 0)

        @pl.when(ch < chunks - 1)
        def _():
            start(x_copies(ch + 1))

        def down(n, _):
            slot = lax.rem(base + ng + n, 2)
            wait(d_copies(n, slot))

            @pl.when(n < nd - 1)
            def _():
                start(d_copies(n + 1, 1 - slot))

            @pl.when((n == nd - 1) & (ch < chunks - 1))
            def _():
                start(gu_copies(0, 1 - slot))

            def unit(lo, size):
                acc = jnp.dot(hb[...], wb[slot, :width, lo:lo + size], preferred_element_type=F32)
                snd[n, :, lo:lo + size] = acc[:half].astype(BF)
                own[lax.rem(n, 2), :, lo:lo + size] = acc[half:]

            unit(0, 768)

            @pl.when(n > 0)
            def _():
                chip_sum(ch, n - 1)

            @pl.when((n == 0) & (ch > 0))
            def _():
                finish(ch - 1, nq - 1)
            unit(768, 512)

            @pl.when(ch > 0)
            def _():
                pl.semaphore_wait(pfree, 1)
            term_copy(n).start()
            return 0

        lax.fori_loop(0, nd, down, 0)
        return 0

    lax.fori_loop(0, chunks, chunk, 0)
    chip_sum(chunks - 1, nd - 1)

    def drain(q, _):
        finish(chunks - 1, q)
        return 0

    lax.fori_loop(0, nq, drain, 0)
    for s in range(2):
        here, there = y_copies(0, 0, s)
        here.wait()
        there.wait_send()

    def arrive(i, _):
        there = y.at[rows_at(0, half), pl.ds(0, Q)]
        remote(yb.at[0], there, ysend.at[0], yrecv.at[i], partner).wait_recv()
        return 0

    lax.fori_loop(0, chunks * nq, arrive, 0)


def solution(mesh):
    def step(x, w_gate, w_up, w_down):
        rows, depth = x.shape
        width = w_gate.shape[1]
        half, nd, nq = CHUNK // 2, depth // T, depth // Q
        dma = pltpu.SemaphoreType.DMA
        return pl.pallas_call(
            kernel,
            out_shape=jax.ShapeDtypeStruct((rows, depth), BF),
            in_specs=[pl.BlockSpec(memory_space=pl.ANY)] * 4,
            out_specs=pl.BlockSpec(memory_space=pl.ANY),
            scratch_shapes=[
                pltpu.VMEM((CHUNK, depth), BF),
                pltpu.VMEM((CHUNK, width), BF),
                pltpu.VMEM((2, depth, T), BF),
                pltpu.VMEM((2, half, T), F32),
                pltpu.VMEM((nd, half, T), BF),
                pltpu.VMEM((nd, half, T), BF),
                pltpu.VMEM((nq, half, Q), BF),
                pltpu.VMEM((nq, half, Q), BF),
                pltpu.VMEM((2, half, Q), BF),
                dma((2,)), dma((2, 2)),
                dma((nd,)), dma((nd,)),
                dma((nq,)), dma((nq,)),
                dma((2,)), dma((2,)), dma((rows // CHUNK * nq,)),
                pltpu.SemaphoreType.REGULAR,
                pltpu.SemaphoreType.REGULAR,
            ],
            compiler_params=pltpu.CompilerParams(
                collective_id=0, has_side_effects=True, vmem_limit_bytes=67043328),
            name="mlp",
        )(x, w_gate, w_up, w_down)

    return jax.shard_map(
        step,
        mesh=mesh,
        in_specs=(P("dp", None), P(None, "tp"), P(None, "tp"), P("tp", None)),
        out_specs=P("dp", None),
        check_vma=False,
    )
```

time: 721 us -> 376 us (0.52)
  Pallas kernels: 0 us -> 359 us
  waiting for transfers between devices: 354 us -> 0 us
  matrix products: 337 us -> 0 us
  between operations: 13.4 us -> 0.01 us
    pallas_call x0 -> x1, Pallas kernels: none -> 359 us  [step(): pl.pallas_call(kernel, out_shape=jax.ShapeDtypeStruct((rows, depth), BF),...]
    psum x1 -> x0, waiting for transfers between devices: 354 us -> none  [step(): return lax.psum(term, 'tp')]
    dot_general x3 -> x0, matrix products: 337 us -> none  [the longest x1 117 us: step(): up = jnp.dot(x, w_up, preferred_element_type=jnp.float32)]
  transfers between devices with their start and end apart: 1 -> 0, of which waited for: 1 -> 0; matrix products, arithmetic and copies ran while one was open for 0% -> 0% of each run, Pallas kernels for 0% -> 0%
where the time goes in v1:
time: 376 us
  Pallas kernels  359 us (95%)
  local copies, waits for them, and re-layouts  17.3 us (5%)
    pallas_call x1, Pallas kernels, step(): pl.pallas_call(kernel, out_shape=jax.ShapeDtypeStruct((rows, depth), BF),...  359 us
    unnamed x1, local copies, waits for them, and re-layouts  17.3 us

profile of v1, /device:TPU:0, one launch (start us, length us, event | category | flops | bytes accessed | tf_op | source)
XLA Modules:
  0.0 376.2 jit_solution(13349611981004900085)
XLA Ops:
  0.0 358.9 %mlp.1 = bf16[2048,5120]{1,0:T(8,128)(2,1)} custom-call(bf16[2048,5120]{1,0:T(8,128)(2,1)} %x.1, bf16[5120,4480]{1,0:T(8,128)(2,1)} %wg.1, bf16[5120,4480]{1,0:T(8,128)(2,1)} %wu.1, bf16[4480,5120]{1,0:T(8,128)(2,1)} %wd.1), custom_call_target="tpu_custom_call" | custom-call | tf_op jit(solution)/shard_map/mlp/pallas_call | solution.py:216
  358.9 17.3 %copy.6 = bf16[2048,5120]{1,0:T(8,128)(2,1)} copy(bf16[2048,5120]{1,0:T(8,128)(2,1)} %mlp.1) | data formatting | bytes 41943040

commit v2 on v0

v2 whole, which is shorter than its diff:
```python
import jax
import jax.numpy as jnp
from jax import lax
from jax.experimental import pallas as pl
from jax.experimental.pallas import tpu as pltpu
from jax.sharding import PartitionSpec as P

BF = jnp.bfloat16
F32 = jnp.float32
M0 = 544
G = 640
T = 1280
Q = 640
GPARTS = ((0, 384), (384, 256))
TPARTS = ((0, 768), (768, 512))
QPARTS = ((0, 640), (640, 640))


def kernel(x, wg, wu, wd, y, xb, hb, wb, own, snd, rcv, csum, crcv, yb,
           xsem, wsem, psend, precv, csend, crecv, ylocal, ysend, yrecv, pfree, cfree):
    rows, depth = x.shape
    width = wg.shape[1]
    ng, nd = width // G, depth // T
    nq = 2 * nd
    last = (rows - 1) // M0
    m1 = rows - last * M0
    tp = lax.axis_index("tp")
    core = lax.rem(tp, 2)
    partner = tp + 1 - 2 * core
    peer = lax.rem(tp + 2, 4)

    def remote(src, dst, send, recv, to):
        return pltpu.make_async_remote_copy(
            src_ref=src, dst_ref=dst, send_sem=send, recv_sem=recv,
            device_id={"tp": to}, device_id_type=pl.DeviceIdType.MESH)

    def signal(sem, to):
        pl.semaphore_signal(sem, inc=1, device_id={"tp": to}, device_id_type=pl.DeviceIdType.MESH)

    def at(i, size, tile=128):
        return pl.ds(pl.multiple_of(i, tile), size)

    def x_copies(ch, m):
        h = m // 2
        return [pltpu.make_async_copy(x.at[at(ch * M0 + who * h, h, 16), :],
                                      xb.at[pl.ds(k * h, h), :], xsem.at[k])
                for k, who in enumerate((1 - core, core))]

    def gu_copies(j, slot, part):
        lo, size = GPARTS[part]
        return [pltpu.make_async_copy(w.at[:, at(j * G + lo, size)],
                                      wb.at[slot, :, pl.ds(2 * lo + k * size, size)], wsem.at[slot, part, k])
                for k, w in enumerate((wg, wu))]

    def d_copies(n, slot, part):
        lo, size = TPARTS[part]
        return [pltpu.make_async_copy(wd.at[:, at(n * T + lo, size)],
                                      wb.at[slot, pl.ds(0, width), pl.ds(lo, size)], wsem.at[slot, part, 0])]

    def start(copies):
        for c in copies:
            c.start()

    def wait(copies):
        for c in copies:
            c.wait()

    def term_copy(n, part, h):
        lo, size = TPARTS[part]
        there = (n, pl.ds(0, h), pl.ds(lo, size))
        return remote(snd.at[there], rcv.at[there], psend.at[2 * n + part], precv.at[2 * n + part], partner)

    def sum_copy(n, part, h, parts):
        lo, size = parts[part]
        there = (n, pl.ds(0, h), pl.ds(lo, size))
        return remote(csum.at[there], crcv.at[there], csend.at[2 * n + part], crecv.at[2 * n + part], peer)

    def y_copies(ch, n, part, h, parts):
        lo, size = parts[part]
        s = part
        here = yb.at[s, pl.ds(0, h), pl.ds(0, size)]
        there = y.at[at(ch * M0 + core * h, h, 16), at(n * T + lo, size)]
        return (pltpu.make_async_copy(here, there, ylocal.at[s]),
                remote(here, there, ysend.at[s], yrecv.at[ch * nq + 2 * n + part], partner))

    def y_free(part, h, parts):
        here, there = y_copies(0, 0, part, h, parts)
        here.wait()
        there.wait_send()

    def send_term(n, part, h, first):
        if first is False:
            pl.semaphore_wait(pfree, 1)
        elif first is not True:
            @pl.when(first == 0)
            def _():
                pl.semaphore_wait(pfree, 1)
        term_copy(n, part, h).start()

    def add_chip(n, part, h):
        lo, size = TPARTS[part]
        csum[n, :h, lo:lo + size] = (
            own[lax.rem(n, 2), :h, lo:lo + size] + rcv[n, :h, lo:lo + size].astype(F32)).astype(BF)

    def add_final(n, part, h, parts, cols):
        lo, size = parts[part]
        if cols is None:
            a, b = csum[n, :h, lo:lo + size], crcv[n, :h, lo:lo + size]
        else:
            a, b = csum[n, :h, cols], crcv[n, :h, cols]
        yb[part, :h, :size] = (a.astype(F32) + b.astype(F32)).astype(BF)

    def gate_up(ch, m, hp):
        base = ch * (ng + nd)
        wait(x_copies(ch, m))

        def tile(j, _):
            slot = lax.rem(base + j, 2)
            wait(gu_copies(j, slot, 0))
            if hp:
                wait(gu_copies(j, slot, 1))
            for part in (0, 1):
                @pl.when(j < ng - 1)
                def _():
                    start(gu_copies(j + 1, 1 - slot, part))

                @pl.when(j == ng - 1)
                def _():
                    start(d_copies(0, 1 - slot, part))
            if hp:
                n, part = lax.div(j, 2), lax.rem(j, 2)
                lo = pl.multiple_of(part * Q, 128)
                q = 2 * n + part

                @pl.when(j == 0)
                def _():
                    for p in (0, 1):
                        term_copy(nd - 1, p, hp).wait()
                        add_chip(nd - 1, p, hp)
                        signal(pfree, partner)

                    @pl.when(ch > 1)
                    def _():
                        pl.semaphore_wait(cfree, 2)
                    for p in (0, 1):
                        sum_copy(nd - 1, p, hp, QPARTS).start()
                there = (n, pl.ds(0, hp), pl.ds(lo, Q))
                remote(csum.at[there], crcv.at[there], csend.at[q], crecv.at[q], peer).wait()
                here = yb.at[part, pl.ds(0, hp), pl.ds(0, Q)]
                out = y.at[at((ch - 1) * M0 + core * hp, hp, 16), at(j * Q, Q)]
                copies = (pltpu.make_async_copy(here, out, ylocal.at[part]),
                          remote(here, out, ysend.at[part], yrecv.at[(ch - 1) * nq + j], partner))

                @pl.when((ch > 1) | (j > 1))
                def _():
                    copies[0].wait()
                    copies[1].wait_send()

            def unit(p):
                lo, size = GPARTS[p]
                acc = jnp.dot(xb[:m], wb[slot, :, 2 * lo:2 * (lo + size)], preferred_element_type=F32)
                hb[:m, at(j * G + lo, size)] = (jax.nn.silu(acc[:, :size]) * acc[:, size:]).astype(BF)

            unit(0)
            if hp:
                yb[part, :hp, :Q] = (csum[n, :hp, pl.ds(lo, Q)].astype(F32)
                                     + crcv[n, :hp, pl.ds(lo, Q)].astype(F32)).astype(BF)
            else:
                wait(gu_copies(j, slot, 1))
            unit(1)
            if hp:
                start(copies)
                signal(cfree, peer)
            return 0

        lax.fori_loop(0, ng, tile, 0)

    def final_prev(ch, hp):
        sum_copy(nd - 1, 1, hp, QPARTS).wait()
        y_free(1, hp, QPARTS)
        add_final(nd - 1, 1, hp, QPARTS, None)
        start(y_copies(ch - 1, nd - 1, 1, hp, QPARTS))
        signal(cfree, peer)

    def down(ch, m, hp, end):
        base = ch * (ng + nd) + ng
        h = m // 2

        def tile(n, first_tile):
            slot = lax.rem(base + n, 2)
            for part in (0, 1):
                wait(d_copies(n, slot, part))

            @pl.when(n < nd - 1)
            def _():
                for part in (0, 1):
                    start(d_copies(n + 1, 1 - slot, part))
            if not end:
                for part in (0, 1):
                    @pl.when((n == nd - 1) & (ch < last))
                    def _():
                        start(gu_copies(0, 1 - slot, part))

            def unit(p):
                lo, size = TPARTS[p]
                acc = jnp.dot(hb[:m], wb[slot, :width, lo:lo + size], preferred_element_type=F32)
                snd[n, :h, lo:lo + size] = acc[:h].astype(BF)
                own[lax.rem(n, 2), :h, lo:lo + size] = acc[h:]

            first = False if end else (ch == 0).astype(jnp.int32)

            def credit(k):
                if end:
                    pl.semaphore_wait(cfree, k)
                else:
                    @pl.when(ch > 0)
                    def _():
                        pl.semaphore_wait(cfree, k)

            unit(0)
            send_term(n, 0, h, first)
            if first_tile:
                if end:
                    final_prev(ch, hp)
                else:
                    @pl.when(ch > 0)
                    def _():
                        final_prev(ch, hp)
            elif end:
                term_copy(n - 1, 1, h).wait()
                add_chip(n - 1, 1, h)
                sum_copy(n - 1, 1, h, TPARTS).start()
            else:
                for p in (0, 1):
                    term_copy(n - 1, p, h).wait()
                for p in (0, 1):
                    add_chip(n - 1, p, h)
            unit(1)
            send_term(n, 1, h, first)
            if end:
                term_copy(n, 0, h).wait()
                add_chip(n, 0, h)
                credit(2)
                sum_copy(n, 0, h, TPARTS).start()
            elif not first_tile:
                for _ in (0, 1):
                    signal(pfree, partner)
                credit(2)
                for p in (0, 1):
                    sum_copy(n - 1, p, h, QPARTS).start()

        def loop(n, _):
            tile(n, False)
            return 0

        tile(0, True)
        lax.fori_loop(1, nd, loop, 0)

    h0, h1 = M0 // 2, m1 // 2
    start(x_copies(0, M0))
    for part in (0, 1):
        start(gu_copies(0, 0, part))
    barrier = pltpu.get_barrier_semaphore()
    signal(barrier, partner)
    signal(barrier, peer)
    pl.semaphore_wait(barrier, 2)

    gate_up(0, M0, None)

    def chunk(ch, _):
        @pl.when(ch < last - 1)
        def _():
            start(x_copies(ch + 1, M0))

        @pl.when(ch == last - 1)
        def _():
            start(x_copies(last, m1))
        down(ch, M0, h0, False)

        @pl.when(ch < last - 1)
        def _():
            gate_up(ch + 1, M0, h0)

        @pl.when(ch == last - 1)
        def _():
            gate_up(ch + 1, m1, h0)
        return 0

    lax.fori_loop(0, last, chunk, 0)
    down(last, m1, h0, True)
    term_copy(nd - 1, 1, h1).wait()
    add_chip(nd - 1, 1, h1)
    sum_copy(nd - 1, 1, h1, TPARTS).start()
    for n in range(nd):
        for part in (0, 1):
            sum_copy(n, part, h1, TPARTS).wait()
            if n == 0:
                y_free(part, h0, QPARTS)
            else:
                y_free(part, h1, TPARTS)
            add_final(n, part, h1, TPARTS, None)
            start(y_copies(last, n, part, h1, TPARTS))
    for part in (0, 1):
        y_free(part, h1, TPARTS)

    def arrive(i, _):
        there = y.at[pl.ds(0, h0), pl.ds(0, Q)]
        remote(yb.at[0, pl.ds(0, h0), pl.ds(0, Q)], there, ysend.at[0], yrecv.at[i], partner).wait_recv()
        return 0

    lax.fori_loop(0, last * nq, arrive, 0)
    for n in range(nd):
        for part in (0, 1):
            y_copies(last, n, part, h1, TPARTS)[1].wait_recv()


def solution(mesh):
    def step(x, w_gate, w_up, w_down):
        rows, depth = x.shape
        width = w_gate.shape[1]
        half, nd = M0 // 2, depth // T
        dma = pltpu.SemaphoreType.DMA
        return pl.pallas_call(
            kernel,
            out_shape=jax.ShapeDtypeStruct((rows, depth), BF),
            in_specs=[pl.BlockSpec(memory_space=pl.ANY)] * 4,
            out_specs=pl.BlockSpec(memory_space=pl.ANY),
            scratch_shapes=[
                pltpu.VMEM((M0, depth), BF),
                pltpu.VMEM((M0, width), BF),
                pltpu.VMEM((2, depth, T), BF),
                pltpu.VMEM((2, half, T), F32),
                pltpu.VMEM((nd, half, T), BF),
                pltpu.VMEM((nd, half, T), BF),
                pltpu.VMEM((nd, half, T), BF),
                pltpu.VMEM((nd, half, T), BF),
                pltpu.VMEM((2, half, TPARTS[0][1]), BF),
                dma((2,)), dma((2, 2, 2)),
                dma((2 * nd,)), dma((2 * nd,)),
                dma((2 * nd,)), dma((2 * nd,)),
                dma((2,)), dma((2,)), dma((-(-rows // M0) * 2 * nd,)),
                pltpu.SemaphoreType.REGULAR,
                pltpu.SemaphoreType.REGULAR,
            ],
            compiler_params=pltpu.CompilerParams(
                collective_id=0, has_side_effects=True, vmem_limit_bytes=67043328),
            name="mlp",
        )(x, w_gate, w_up, w_down)

    return jax.shard_map(
        step,
        mesh=mesh,
        in_specs=(P("dp", None), P(None, "tp"), P(None, "tp"), P("tp", None)),
        out_specs=P("dp", None),
        check_vma=False,
    )
```

time: 721 us -> 369 us (0.51)
  waiting for transfers between devices: 354 us -> 0 us
  Pallas kernels: 0 us -> 352 us
  matrix products: 337 us -> 0 us
  between operations: 13.4 us -> 0.01 us
    psum x1 -> x0, waiting for transfers between devices: 354 us -> none  [step(): return lax.psum(term, 'tp')]
    pallas_call x0 -> x1, Pallas kernels: none -> 352 us  [step(): pl.pallas_call(kernel, out_shape=jax.ShapeDtypeStruct((rows, depth), BF),...]
    dot_general x3 -> x0, matrix products: 337 us -> none  [the longest x1 117 us: step(): up = jnp.dot(x, w_up, preferred_element_type=jnp.float32)]
  transfers between devices with their start and end apart: 1 -> 0, of which waited for: 1 -> 0; matrix products, arithmetic and copies ran while one was open for 0% -> 0% of each run, Pallas kernels for 0% -> 0%
where the time goes in v2:
time: 369 us
  Pallas kernels  352 us (95%)
  local copies, waits for them, and re-layouts  17.3 us (5%)
    pallas_call x1, Pallas kernels, step(): pl.pallas_call(kernel, out_shape=jax.ShapeDtypeStruct((rows, depth), BF),...  352 us
    unnamed x1, local copies, waits for them, and re-layouts  17.3 us

profile of v2, /device:TPU:0, one launch (start us, length us, event | category | flops | bytes accessed | tf_op | source)
XLA Modules:
  0.0 369.1 jit_solution(11160835391046152404)
XLA Ops:
  0.0 351.7 %mlp.1 = bf16[2048,5120]{1,0:T(8,128)(2,1)} custom-call(bf16[2048,5120]{1,0:T(8,128)(2,1)} %x.1, bf16[5120,4480]{1,0:T(8,128)(2,1)} %wg.1, bf16[5120,4480]{1,0:T(8,128)(2,1)} %wu.1, bf16[4480,5120]{1,0:T(8,128)(2,1)} %wd.1), custom_call_target="tpu_custom_call" | custom-call | tf_op jit(solution)/shard_map/mlp/pallas_call | solution.py:323
  351.8 17.3 %copy.6 = bf16[2048,5120]{1,0:T(8,128)(2,1)} copy(bf16[2048,5120]{1,0:T(8,128)(2,1)} %mlp.1) | data formatting | bytes 41943040

commit v3 on v2

--- a/solution.py
+++ b/solution.py
@@ -7,7 +7,7 @@
 
 BF = jnp.bfloat16
 F32 = jnp.float32
-M0 = 544
+M0 = 576
 G = 640
 T = 1280
 Q = 640
@@ -16,8 +16,8 @@
 QPARTS = ((0, 640), (640, 640))
 
 
-def kernel(x, wg, wu, wd, y, xb, hb, wb, own, snd, rcv, csum, crcv, yb,
-           xsem, wsem, psend, precv, csend, crecv, ylocal, ysend, yrecv, pfree, cfree):
+def kernel(x, wg, wu, wd, y, wb, xb, hb, own, snd, rcv, csum, crcv, yb,
+           xsem, wsem, psend, precv, csend, crecv, ylocal, ysend, yrecv, vsem, pfree, cfree, vfree):
     rows, depth = x.shape
     width = wg.shape[1]
     ng, nd = width // G, depth // T
@@ -83,6 +83,19 @@
         return (pltpu.make_async_copy(here, there, ylocal.at[s]),
                 remote(here, there, ysend.at[s], yrecv.at[ch * nq + 2 * n + part], partner))
 
+    def spot(n, row, size):
+        return n // 2, at((n % 2) * rows + row, size, 16)
+
+    def end_copy(n, part, h):
+        lo, size = TPARTS[part]
+        slot, there = spot(n, last * M0 + core * h, h)
+        here = wb.at[slot, there, pl.ds(lo, size)]
+        return remote(here, here, csend.at[2 * n + part], yrecv.at[last * nq + 2 * n + part], partner)
+
+    def load_copies(n):
+        slot, there = spot(n, 0, last * M0)
+        return pltpu.make_async_copy(y.at[:, pl.ds(n * T, T)], wb.at[slot, there, :], vsem.at[n])
+
     def y_free(part, h, parts):
         here, there = y_copies(0, 0, part, h, parts)
         here.wait()
@@ -110,40 +123,38 @@
             a, b = csum[n, :h, cols], crcv[n, :h, cols]
         yb[part, :h, :size] = (a.astype(F32) + b.astype(F32)).astype(BF)
 
-    def gate_up(ch, m, hp):
+    def gate_up(ch, m, hp, ahead):
         base = ch * (ng + nd)
         wait(x_copies(ch, m))
+        split = ahead or not hp
 
         def tile(j, _):
             slot = lax.rem(base + j, 2)
             wait(gu_copies(j, slot, 0))
-            if hp:
+            if not split:
                 wait(gu_copies(j, slot, 1))
-            for part in (0, 1):
-                @pl.when(j < ng - 1)
-                def _():
-                    start(gu_copies(j + 1, 1 - slot, part))
-
-                @pl.when(j == ng - 1)
-                def _():
-                    start(d_copies(0, 1 - slot, part))
+
+            def fetch(tile_no, where, part):
+                @pl.when(tile_no < ng)
+                def _():
+                    start(gu_copies(tile_no, where, part))
+
+                @pl.when(tile_no >= ng)
+                def _():
+                    start(d_copies(tile_no - ng, where, part))
+
+            if ahead:
+                @pl.when(j == 0)
+                def _():
+                    for part in (0, 1):
+                        start(gu_copies(1, 1 - slot, part))
+            else:
+                for part in (0, 1):
+                    fetch(j + 1, 1 - slot, part)
             if hp:
                 n, part = lax.div(j, 2), lax.rem(j, 2)
                 lo = pl.multiple_of(part * Q, 128)
                 q = 2 * n + part
-
-                @pl.when(j == 0)
-                def _():
-                    for p in (0, 1):
-                        term_copy(nd - 1, p, hp).wait()
-                        add_chip(nd - 1, p, hp)
-                        signal(pfree, partner)
-
-                    @pl.when(ch > 1)
-                    def _():
-                        pl.semaphore_wait(cfree, 2)
-                    for p in (0, 1):
-                        sum_copy(nd - 1, p, hp, QPARTS).start()
                 there = (n, pl.ds(0, hp), pl.ds(lo, Q))
                 remote(csum.at[there], crcv.at[there], csend.at[q], crecv.at[q], peer).wait()
                 here = yb.at[part, pl.ds(0, hp), pl.ds(0, Q)]
@@ -158,16 +169,37 @@
 
             def unit(p):
                 lo, size = GPARTS[p]
-                acc = jnp.dot(xb[:m], wb[slot, :, 2 * lo:2 * (lo + size)], preferred_element_type=F32)
-                hb[:m, at(j * G + lo, size)] = (jax.nn.silu(acc[:, :size]) * acc[:, size:]).astype(BF)
+                for k in range(0, size, 128):
+                    w = jnp.concatenate([wb[slot, :, c:c + 128] for c in (2 * lo + k, 2 * lo + size + k)], axis=1)
+                    acc = jnp.dot(xb[:m], w, preferred_element_type=F32)
+                    hb[:m, at(j * G + lo + k, 128)] = (jax.nn.silu(acc[:, :128]) * acc[:, 128:]).astype(BF)
 
             unit(0)
+            if ahead:
+                fetch(j + 2, slot, 0)
+            if hp:
+                @pl.when(j == 0)
+                def _():
+                    for p in (0, 1):
+                        term_copy(nd - 1, p, hp).wait()
+                        add_chip(nd - 1, p, hp)
+
+                    for _ in (0, 1):
+                        signal(pfree, partner)
+
+                    @pl.when(ch > 1)
+                    def _():
+                        pl.semaphore_wait(cfree, 2)
+                    for p in (0, 1):
+                        sum_copy(nd - 1, p, hp, QPARTS).start()
+            if split:
+                wait(gu_copies(j, slot, 1))
             if hp:
                 yb[part, :hp, :Q] = (csum[n, :hp, pl.ds(lo, Q)].astype(F32)
                                      + crcv[n, :hp, pl.ds(lo, Q)].astype(F32)).astype(BF)
-            else:
-                wait(gu_copies(j, slot, 1))
             unit(1)
+            if ahead:
+                fetch(j + 2, slot, 1)
             if hp:
                 start(copies)
                 signal(cfree, peer)
@@ -191,21 +223,26 @@
             for part in (0, 1):
                 wait(d_copies(n, slot, part))
 
-            @pl.when(n < nd - 1)
-            def _():
-                for part in (0, 1):
-                    start(d_copies(n + 1, 1 - slot, part))
+            def fetch(tile_no, where, part):
+                @pl.when(tile_no < nd)
+                def _():
+                    start(d_copies(tile_no, where, part))
+
+                if not end:
+                    @pl.when(tile_no >= nd)
+                    def _():
+                        start(gu_copies(tile_no - nd, where, part))
+
             if not end:
                 for part in (0, 1):
-                    @pl.when((n == nd - 1) & (ch < last))
-                    def _():
-                        start(gu_copies(0, 1 - slot, part))
+                    fetch(n + 1, 1 - slot, part)
 
             def unit(p):
                 lo, size = TPARTS[p]
-                acc = jnp.dot(hb[:m], wb[slot, :width, lo:lo + size], preferred_element_type=F32)
-                snd[n, :h, lo:lo + size] = acc[:h].astype(BF)
-                own[lax.rem(n, 2), :h, lo:lo + size] = acc[h:]
+                for c in range(lo, lo + size, 256):
+                    acc = jnp.dot(hb[:m], wb[slot, :width, c:c + 256], preferred_element_type=F32)
+                    snd[n, :h, c:c + 256] = acc[:h].astype(BF)
+                    own[lax.rem(n, 2), :h, c:c + 256] = acc[h:]
 
             first = False if end else (ch == 0).astype(jnp.int32)
 
@@ -218,7 +255,9 @@
                         pl.semaphore_wait(cfree, k)
 
             unit(0)
-            send_term(n, 0, h, first)
+            if end:
+                fetch(n + 2, slot, 0)
+                send_term(n, 0, h, first)
             if first_tile:
                 if end:
                     final_prev(ch, hp)
@@ -236,18 +275,22 @@
                 for p in (0, 1):
                     add_chip(n - 1, p, h)
             unit(1)
-            send_term(n, 1, h, first)
             if end:
+                fetch(n + 2, slot, 1)
+                send_term(n, 1, h, first)
                 term_copy(n, 0, h).wait()
                 add_chip(n, 0, h)
                 credit(2)
                 sum_copy(n, 0, h, TPARTS).start()
-            elif not first_tile:
-                for _ in (0, 1):
-                    signal(pfree, partner)
-                credit(2)
+            else:
                 for p in (0, 1):
-                    sum_copy(n - 1, p, h, QPARTS).start()
+                    send_term(n, p, h, first)
+                if not first_tile:
+                    for _ in (0, 1):
+                        signal(pfree, partner)
+                    credit(2)
+                    for p in (0, 1):
+                        sum_copy(n - 1, p, h, QPARTS).start()
 
         def loop(n, _):
             tile(n, False)
@@ -265,7 +308,7 @@
     signal(barrier, peer)
     pl.semaphore_wait(barrier, 2)
 
-    gate_up(0, M0, None)
+    gate_up(0, M0, None, False)
 
     def chunk(ch, _):
         @pl.when(ch < last - 1)
@@ -279,29 +322,21 @@
 
         @pl.when(ch < last - 1)
         def _():
-            gate_up(ch + 1, M0, h0)
+            gate_up(ch + 1, M0, h0, False)
 
         @pl.when(ch == last - 1)
         def _():
-            gate_up(ch + 1, m1, h0)
+            gate_up(ch + 1, m1, h0, True)
         return 0
 
     lax.fori_loop(0, last, chunk, 0)
     down(last, m1, h0, True)
+    signal(vfree, partner)
     term_copy(nd - 1, 1, h1).wait()
     add_chip(nd - 1, 1, h1)
     sum_copy(nd - 1, 1, h1, TPARTS).start()
-    for n in range(nd):
-        for part in (0, 1):
-            sum_copy(n, part, h1, TPARTS).wait()
-            if n == 0:
-                y_free(part, h0, QPARTS)
-            else:
-                y_free(part, h1, TPARTS)
-            add_final(n, part, h1, TPARTS, None)
-            start(y_copies(last, n, part, h1, TPARTS))
     for part in (0, 1):
-        y_free(part, h1, TPARTS)
+        y_free(part, h0, QPARTS)
 
     def arrive(i, _):
         there = y.at[pl.ds(0, h0), pl.ds(0, Q)]
@@ -310,8 +345,35 @@
 
     lax.fori_loop(0, last * nq, arrive, 0)
     for n in range(nd):
+        load_copies(n).start()
+    pl.semaphore_wait(vfree, 1)
+    for n in range(nd):
         for part in (0, 1):
-            y_copies(last, n, part, h1, TPARTS)[1].wait_recv()
+            lo, size = TPARTS[part]
+            sum_copy(n, part, h1, TPARTS).wait()
+            slot, there = spot(n, last * M0 + core * h1, h1)
+            wb[slot, there, lo:lo + size] = (csum[n, :h1, lo:lo + size].astype(F32)
+                                             + crcv[n, :h1, lo:lo + size].astype(F32)).astype(BF)
+            end_copy(n, part, h1).start()
+    for n in range(nd):
+        load_copies(n).wait()
+        for part in (0, 1):
+            end_copy(n, part, h1).wait()
+
+
+def unload(v, y, sem):
+    rows, depth = y.shape
+    cuts = 2
+    copies = []
+    for n in range(depth // T):
+        for k in range(cuts):
+            r = rows // cuts
+            src = v.at[n // 2, pl.ds((n % 2) * rows + k * r, r), :]
+            copies.append(pltpu.make_async_copy(src, y.at[pl.ds(k * r, r), pl.ds(n * T, T)], sem.at[cuts * n + k]))
+    for c in copies:
+        c.start()
+    for c in copies:
+        c.wait()
 
 
 def solution(mesh):
@@ -320,32 +382,44 @@
         width = w_gate.shape[1]
         half, nd = M0 // 2, depth // T
         dma = pltpu.SemaphoreType.DMA
-        return pl.pallas_call(
+        any_space, vmem = pl.BlockSpec(memory_space=pl.ANY), pl.BlockSpec(memory_space=pltpu.VMEM)
+        last = (rows - 1) // M0
+        _, held = pl.pallas_call(
             kernel,
-            out_shape=jax.ShapeDtypeStruct((rows, depth), BF),
-            in_specs=[pl.BlockSpec(memory_space=pl.ANY)] * 4,
-            out_specs=pl.BlockSpec(memory_space=pl.ANY),
+            out_shape=(jax.ShapeDtypeStruct((last * M0, depth), BF), pltpu.VMEM((2, depth, T), BF)),
+            in_specs=[any_space] * 4,
+            out_specs=(any_space, vmem),
             scratch_shapes=[
                 pltpu.VMEM((M0, depth), BF),
                 pltpu.VMEM((M0, width), BF),
-                pltpu.VMEM((2, depth, T), BF),
                 pltpu.VMEM((2, half, T), F32),
                 pltpu.VMEM((nd, half, T), BF),
                 pltpu.VMEM((nd, half, T), BF),
                 pltpu.VMEM((nd, half, T), BF),
                 pltpu.VMEM((nd, half, T), BF),
-                pltpu.VMEM((2, half, TPARTS[0][1]), BF),
+                pltpu.VMEM((2, half, Q), BF),
                 dma((2,)), dma((2, 2, 2)),
                 dma((2 * nd,)), dma((2 * nd,)),
                 dma((2 * nd,)), dma((2 * nd,)),
-                dma((2,)), dma((2,)), dma((-(-rows // M0) * 2 * nd,)),
+                dma((2,)), dma((2,)), dma(((last + 1) * 2 * nd,)), dma((nd,)),
+                pltpu.SemaphoreType.REGULAR,
                 pltpu.SemaphoreType.REGULAR,
                 pltpu.SemaphoreType.REGULAR,
             ],
             compiler_params=pltpu.CompilerParams(
-                collective_id=0, has_side_effects=True, vmem_limit_bytes=67043328),
+                collective_id=0, has_side_effects=True, vmem_limit_bytes=40000000),
             name="mlp",
         )(x, w_gate, w_up, w_down)
+        held = pltpu.with_memory_space_constraint(held, pltpu.VMEM)
+        return pl.pallas_call(
+            unload,
+            out_shape=jax.ShapeDtypeStruct((rows, depth), BF),
+            in_specs=[vmem],
+            out_specs=any_space,
+            scratch_shapes=[dma((2 * nd,))],
+            compiler_params=pltpu.CompilerParams(vmem_limit_bytes=4000000),
+            name="unload",
+        )(held)
 
     return jax.shard_map(
         step,

time: 369 us -> 367 us (level)
  local copies, waits for them, and re-layouts: 17.3 us -> 0 us
  Pallas kernels: 352 us -> 367 us
    unnamed x1 -> x0, local copies, waits for them, and re-layouts: 17.3 us -> none
    pallas_call x1 -> x2, Pallas kernels: 352 us -> 367 us  [the longest x1 359 us: step(): pl.pallas_call(kernel, out_shape=(jax.ShapeDtypeStruct((last * M0, depth)...]
where the time goes in v3:
time: 367 us
  Pallas kernels  367 us (100%)
    pallas_call x1, Pallas kernels, step(): pl.pallas_call(kernel, out_shape=(jax.ShapeDtypeStruct((last * M0, depth)...  359 us

profile of v3, /device:TPU:0, one launch (start us, length us, event | category | flops | bytes accessed | tf_op | source)
XLA Modules:
  0.0 366.7 jit_solution(3190100599627666170)
XLA Ops:
  0.0 359.3 %mlp.1 = (bf16[1728,5120]{1,0:T(8,128)(2,1)}, bf16[2,5120,1280]{2,1,0:T(8,128)(2,1)S(1)}) custom-call(bf16[2048,5120]{1,0:T(8,128)(2,1)} %x.1, bf16[5120,4480]{1,0:T(8,128)(2,1)} %wg.1, bf16[5120,4480]{1,0:T(8,128)(2,1)} %wu.1, bf16[4480,5120]{1,0:T(8,128)(2,1)} %wd.1), custom_call_target="tpu_custom_call" | custom-call | tf_op jit(solution)/shard_map/mlp/pallas_call | solution.py:387
  359.3 7.2 %unload.1 = bf16[2048,5120]{1,0:T(8,128)(2,1)} custom-call(bf16[2,5120,1280]{2,1,0:T(8,128)(2,1)S(1)} %get-tuple-element.6.v), custom_call_target="tpu_custom_call" | custom-call | tf_op jit(solution)/shard_map/unload/pallas_call | solution.py:414

commit v4 on v3

--- a/solution.py
+++ b/solution.py
@@ -7,7 +7,7 @@
 
 BF = jnp.bfloat16
 F32 = jnp.float32
-M0 = 576
+M0 = 544
 G = 640
 T = 1280
 Q = 640
@@ -123,16 +123,14 @@
             a, b = csum[n, :h, cols], crcv[n, :h, cols]
         yb[part, :h, :size] = (a.astype(F32) + b.astype(F32)).astype(BF)
 
-    def gate_up(ch, m, hp, ahead):
+    def gate_up(ch, m, hp, late):
         base = ch * (ng + nd)
         wait(x_copies(ch, m))
-        split = ahead or not hp
 
         def tile(j, _):
             slot = lax.rem(base + j, 2)
-            wait(gu_copies(j, slot, 0))
-            if not split:
-                wait(gu_copies(j, slot, 1))
+            for part in (0, 1):
+                wait(gu_copies(j, slot, part))
 
             def fetch(tile_no, where, part):
                 @pl.when(tile_no < ng)
@@ -143,29 +141,29 @@
                 def _():
                     start(d_copies(tile_no - ng, where, part))
 
-            if ahead:
-                @pl.when(j == 0)
-                def _():
-                    for part in (0, 1):
-                        start(gu_copies(1, 1 - slot, part))
-            else:
-                for part in (0, 1):
-                    fetch(j + 1, 1 - slot, part)
+            for part in (0, 1):
+                fetch(j + 1, 1 - slot, part)
             if hp:
                 n, part = lax.div(j, 2), lax.rem(j, 2)
                 lo = pl.multiple_of(part * Q, 128)
                 q = 2 * n + part
                 there = (n, pl.ds(0, hp), pl.ds(lo, Q))
-                remote(csum.at[there], crcv.at[there], csend.at[q], crecv.at[q], peer).wait()
                 here = yb.at[part, pl.ds(0, hp), pl.ds(0, Q)]
                 out = y.at[at((ch - 1) * M0 + core * hp, hp, 16), at(j * Q, Q)]
                 copies = (pltpu.make_async_copy(here, out, ylocal.at[part]),
                           remote(here, out, ysend.at[part], yrecv.at[(ch - 1) * nq + j], partner))
 
+            def ready():
+                remote(csum.at[there], crcv.at[there], csend.at[q], crecv.at[q], peer).wait()
+
                 @pl.when((ch > 1) | (j > 1))
                 def _():
                     copies[0].wait()
                     copies[1].wait_send()
+
+            def add():
+                yb[part, :hp, :Q] = (csum[n, :hp, pl.ds(lo, Q)].astype(F32)
+                                     + crcv[n, :hp, pl.ds(lo, Q)].astype(F32)).astype(BF)
 
             def unit(p):
                 lo, size = GPARTS[p]
@@ -174,9 +172,12 @@
                     acc = jnp.dot(xb[:m], w, preferred_element_type=F32)
                     hb[:m, at(j * G + lo + k, 128)] = (jax.nn.silu(acc[:, :128]) * acc[:, 128:]).astype(BF)
 
+            if hp and not late:
+                ready()
             unit(0)
-            if ahead:
-                fetch(j + 2, slot, 0)
+            if hp and not late:
+                add()
+            unit(1)
             if hp:
                 @pl.when(j == 0)
                 def _():
@@ -192,15 +193,9 @@
                         pl.semaphore_wait(cfree, 2)
                     for p in (0, 1):
                         sum_copy(nd - 1, p, hp, QPARTS).start()
-            if split:
-                wait(gu_copies(j, slot, 1))
-            if hp:
-                yb[part, :hp, :Q] = (csum[n, :hp, pl.ds(lo, Q)].astype(F32)
-                                     + crcv[n, :hp, pl.ds(lo, Q)].astype(F32)).astype(BF)
-            unit(1)
-            if ahead:
-                fetch(j + 2, slot, 1)
-            if hp:
+                if late:
+                    ready()
+                    add()
                 start(copies)
                 signal(cfree, peer)
             return 0
@@ -233,9 +228,8 @@
                     def _():
                         start(gu_copies(tile_no - nd, where, part))
 
-            if not end:
-                for part in (0, 1):
-                    fetch(n + 1, 1 - slot, part)
+            for part in (0, 1):
+                fetch(n + 1, 1 - slot, part)
 
             def unit(p):
                 lo, size = TPARTS[p]
@@ -256,12 +250,9 @@
 
             unit(0)
             if end:
-                fetch(n + 2, slot, 0)
                 send_term(n, 0, h, first)
             if first_tile:
-                if end:
-                    final_prev(ch, hp)
-                else:
+                if not end:
                     @pl.when(ch > 0)
                     def _():
                         final_prev(ch, hp)
@@ -269,6 +260,10 @@
                 term_copy(n - 1, 1, h).wait()
                 add_chip(n - 1, 1, h)
                 sum_copy(n - 1, 1, h, TPARTS).start()
+
+                @pl.when(n == 1)
+                def _():
+                    final_prev(ch, hp)
             else:
                 for p in (0, 1):
                     term_copy(n - 1, p, h).wait()
@@ -276,7 +271,6 @@
                     add_chip(n - 1, p, h)
             unit(1)
             if end:
-                fetch(n + 2, slot, 1)
                 send_term(n, 1, h, first)
                 term_copy(n, 0, h).wait()
                 add_chip(n, 0, h)

time: 367 us -> 359 us (0.978)
  Pallas kernels: 367 us -> 359 us
    pallas_call x1, Pallas kernels: 359 us -> 352 us  [step(): pl.pallas_call(kernel, out_shape=(jax.ShapeDtypeStruct((last * M0, depth)...]
where the time goes in v4:
time: 359 us
  Pallas kernels  359 us (100%)
    pallas_call x1, Pallas kernels, step(): pl.pallas_call(kernel, out_shape=(jax.ShapeDtypeStruct((last * M0, depth)...  352 us
    pallas_call x1, Pallas kernels, step(): pl.pallas_call(unload, out_shape=jax.ShapeDtypeStruct((rows, depth), BF),...  7.23 us

profile of v4, /device:TPU:0, one launch (start us, length us, event | category | flops | bytes accessed | tf_op | source)
XLA Modules:
  0.0 359.4 jit_solution(5391175118996484307)
XLA Ops:
  0.0 352.0 %mlp.1 = (bf16[1632,5120]{1,0:T(8,128)(2,1)}, bf16[2,5120,1280]{2,1,0:T(8,128)(2,1)S(1)}) custom-call(bf16[2048,5120]{1,0:T(8,128)(2,1)} %x.1, bf16[5120,4480]{1,0:T(8,128)(2,1)} %wg.1, bf16[5120,4480]{1,0:T(8,128)(2,1)} %wu.1, bf16[4480,5120]{1,0:T(8,128)(2,1)} %wd.1), custom_call_target="tpu_custom_call" | custom-call | tf_op jit(solution)/shard_map/mlp/pallas_call | solution.py:381
  352.0 7.2 %unload.1 = bf16[2048,5120]{1,0:T(8,128)(2,1)} custom-call(bf16[2,5120,1280]{2,1,0:T(8,128)(2,1)S(1)} %get-tuple-element.6.v), custom_call_target="tpu_custom_call" | custom-call | tf_op jit(solution)/shard_map/unload/pallas_call | solution.py:408

commit v5 on v4

--- a/solution.py
+++ b/solution.py
@@ -7,7 +7,7 @@
 
 BF = jnp.bfloat16
 F32 = jnp.float32
-M0 = 544
+M0 = 512
 G = 640
 T = 1280
 Q = 640
@@ -305,22 +305,28 @@
     gate_up(0, M0, None, False)
 
     def chunk(ch, _):
-        @pl.when(ch < last - 1)
-        def _():
+        if m1 == M0:
             start(x_copies(ch + 1, M0))
-
-        @pl.when(ch == last - 1)
-        def _():
-            start(x_copies(last, m1))
+        else:
+            @pl.when(ch < last - 1)
+            def _():
+                start(x_copies(ch + 1, M0))
+
+            @pl.when(ch == last - 1)
+            def _():
+                start(x_copies(last, m1))
         down(ch, M0, h0, False)
 
-        @pl.when(ch < last - 1)
-        def _():
+        if m1 == M0:
             gate_up(ch + 1, M0, h0, False)
-
-        @pl.when(ch == last - 1)
-        def _():
-            gate_up(ch + 1, m1, h0, True)
+        else:
+            @pl.when(ch < last - 1)
+            def _():
+                gate_up(ch + 1, M0, h0, False)
+
+            @pl.when(ch == last - 1)
+            def _():
+                gate_up(ch + 1, m1, h0, True)
         return 0
 
     lax.fori_loop(0, last, chunk, 0)

time: 359 us -> 364 us (1.014)
  Pallas kernels: 359 us -> 364 us
    pallas_call x1, Pallas kernels: 352 us -> 357 us  [step(): pl.pallas_call(kernel, out_shape=(jax.ShapeDtypeStruct((last * M0, depth)...]
where the time goes in v5:
time: 364 us
  Pallas kernels  364 us (100%)
    pallas_call x1, Pallas kernels, step(): pl.pallas_call(kernel, out_shape=(jax.ShapeDtypeStruct((last * M0, depth)...  357 us

profile of v5, /device:TPU:0, one launch (start us, length us, event | category | flops | bytes accessed | tf_op | source)
XLA Modules:
  0.0 364.2 jit_solution(16512331454503922031)
XLA Ops:
  0.0 356.8 %mlp.1 = (bf16[1536,5120]{1,0:T(8,128)(2,1)}, bf16[2,5120,1280]{2,1,0:T(8,128)(2,1)S(1)}) custom-call(bf16[2048,5120]{1,0:T(8,128)(2,1)} %x.1, bf16[5120,4480]{1,0:T(8,128)(2,1)} %wg.1, bf16[5120,4480]{1,0:T(8,128)(2,1)} %wu.1, bf16[4480,5120]{1,0:T(8,128)(2,1)} %wd.1), custom_call_target="tpu_custom_call" | custom-call | tf_op jit(solution)/shard_map/mlp/pallas_call | solution.py:387
  356.8 7.2 %unload.1 = bf16[2048,5120]{1,0:T(8,128)(2,1)} custom-call(bf16[2,5120,1280]{2,1,0:T(8,128)(2,1)S(1)} %get-tuple-element.6.v), custom_call_target="tpu_custom_call" | custom-call | tf_op jit(solution)/shard_map/unload/pallas_call | solution.py:414

commit v6 on v4

--- a/solution.py
+++ b/solution.py
@@ -129,8 +129,9 @@
 
         def tile(j, _):
             slot = lax.rem(base + j, 2)
-            for part in (0, 1):
-                wait(gu_copies(j, slot, part))
+            opening = isinstance(j, int)
+            wait(gu_copies(j, slot, 0))
+            (start if opening else wait)(gu_copies(j, slot, 1))
 
             def fetch(tile_no, where, part):
                 @pl.when(tile_no < ng)
@@ -177,6 +178,8 @@
             unit(0)
             if hp and not late:
                 add()
+            if opening:
+                wait(gu_copies(j, slot, 1))
             unit(1)
             if hp:
                 @pl.when(j == 0)
@@ -200,7 +203,9 @@
                 signal(cfree, peer)
             return 0
 
-        lax.fori_loop(0, ng, tile, 0)
+        if not hp:
+            tile(0, 0)
+        lax.fori_loop(0 if hp else 1, ng, tile, 0)
 
     def final_prev(ch, hp):
         sum_copy(nd - 1, 1, hp, QPARTS).wait()
@@ -295,8 +300,7 @@
 
     h0, h1 = M0 // 2, m1 // 2
     start(x_copies(0, M0))
-    for part in (0, 1):
-        start(gu_copies(0, 0, part))
+    start(gu_copies(0, 0, 0))
     barrier = pltpu.get_barrier_semaphore()
     signal(barrier, partner)
     signal(barrier, peer)

time: 359 us -> 358 us (level)
  no operation moved by 1% of the time
where the time goes in v6:
time: 358 us
  Pallas kernels  358 us (100%)
    pallas_call x1, Pallas kernels, step(): pl.pallas_call(kernel, out_shape=(jax.ShapeDtypeStruct((last * M0, depth)...  351 us
    pallas_call x1, Pallas kernels, step(): pl.pallas_call(unload, out_shape=jax.ShapeDtypeStruct((rows, depth), BF),...  7.23 us

profile of v6, /device:TPU:0, one launch (start us, length us, event | category | flops | bytes accessed | tf_op | source)
XLA Modules:
  0.0 358.1 jit_solution(13445716220369197326)
XLA Ops:
  0.0 350.6 %mlp.1 = (bf16[1632,5120]{1,0:T(8,128)(2,1)}, bf16[2,5120,1280]{2,1,0:T(8,128)(2,1)S(1)}) custom-call(bf16[2048,5120]{1,0:T(8,128)(2,1)} %x.1, bf16[5120,4480]{1,0:T(8,128)(2,1)} %wg.1, bf16[5120,4480]{1,0:T(8,128)(2,1)} %wu.1, bf16[4480,5120]{1,0:T(8,128)(2,1)} %wd.1), custom_call_target="tpu_custom_call" | custom-call | tf_op jit(solution)/shard_map/mlp/pallas_call | solution.py:385
  350.7 7.2 %unload.1 = bf16[2048,5120]{1,0:T(8,128)(2,1)} custom-call(bf16[2,5120,1280]{2,1,0:T(8,128)(2,1)S(1)} %get-tuple-element.6.v), custom_call_target="tpu_custom_call" | custom-call | tf_op jit(solution)/shard_map/unload/pallas_call | solution.py:412
